TPU v7x, 32 devices: a 4x4x1 block of a 4x4x8 slice. The times are simulated.
32 devices in a mesh: dp: 1 (over z), tp: 4 (over y), fsdp: 8 (over x, core).
Axes of the slice: x: 4, y: 4, z: 1, core: 2. Of those that a mesh axis runs over, the one named last changes fastest.
The devices are a block of a 4x4x8 slice.
Arguments:
- tokens: int32 [128, 2048], P(('dp', 'fsdp'))
- out_grad: bfloat16 [128, 2048, 1024], P(('dp', 'fsdp'))
- head_grad: float32 [32128, 1024], P(('dp', 'tp'), 'fsdp')
- master_w: float32 [32128, 1024], P(('dp', 'tp'), 'fsdp')
- moment_m: float32 [32128, 1024], P(('dp', 'tp'), 'fsdp')
- moment_v: float32 [32128, 1024], P(('dp', 'tp'), 'fsdp')
- learn_rate: float32 [], replicated
- clip_scale: float32 [], replicated
Outputs:
- output 1: float32 [32128, 1024], P(('dp', 'tp'), 'fsdp')
- output 2: float32 [32128, 1024], P(('dp', 'tp'), 'fsdp')
- output 3: float32 [32128, 1024], P(('dp', 'tp'), 'fsdp')
- output 4: bfloat16 [32128, 1024], P(('dp', 'tp'), 'fsdp')
All inputs are finite; a program needn't handle non-finite values.
Results may differ from a plain program's by a relative error of at most 0.001.
Values sent between devices are 32-bit elements.
A program may use at most 768 MiB of HBM per device.

v0:
```python
import jax
import jax.numpy as jnp
from jax import lax
from jax.sharding import PartitionSpec as P

OPT_STEP = 20


def adafactor_update(embed_grad, head_grad, master_w, moment_m, moment_v, learn_rate, clip_scale):
    beta_two = 1.0 - OPT_STEP ** -0.8
    grad_full = clip_scale * (embed_grad + head_grad)
    new_v = beta_two * moment_v + (1.0 - beta_two) * (grad_full * grad_full + 1e-30)
    new_m = 0.9 * moment_m + 0.1 * (grad_full / jnp.sqrt(new_v))
    new_w = master_w - learn_rate * new_m - learn_rate * learn_rate * master_w
    return new_w, new_m, new_v, new_w.astype(jnp.bfloat16)


def solution(mesh):
    row_spec = P(("dp", "fsdp"), None)
    act_spec = P(("dp", "fsdp"), None, None)
    table_spec = P(("dp", "tp"), "fsdp")

    def local_step(tokens, out_grad, head_grad, master_w, moment_m, moment_v, learn_rate, clip_scale):
        shard_rows = master_w.shape[0]
        model_dim = out_grad.shape[2]
        local_ids = tokens.reshape(-1) - lax.axis_index("tp") * shard_rows
        seg_ids = jnp.where((local_ids >= 0) & (local_ids < shard_rows), local_ids, shard_rows)
        dense_part = jax.ops.segment_sum(out_grad.reshape(-1, model_dim).astype(jnp.float32), seg_ids, num_segments=shard_rows)
        embed_grad = lax.psum_scatter(dense_part, "fsdp", scatter_dimension=1, tiled=True)
        return adafactor_update(embed_grad, head_grad, master_w, moment_m, moment_v, learn_rate, clip_scale)

    return jax.shard_map(local_step, mesh=mesh, in_specs=(row_spec, act_spec, table_spec, table_spec, table_spec, table_spec, P(), P()), out_specs=(table_spec, table_spec, table_spec, table_spec), check_vma=False)
```

profile of v0, /device:TPU:97, one launch (start us, length us, event | category | flops | bytes accessed | tf_op | source)
XLA Modules:
  0.0 480.8 jit_solution(2867185390267561788)
XLA Ops:
  7.2 0.1 reduce-scatter.2.cloned.1.call-start
  7.3 0.9 subtract_bitcast_fusion
  8.2 0.1 copy.12
  8.3 0.2 and_select_fusion
  8.5 283.1 %scatter_custom_fusion = f32[8032,1024]{1,0:T(8,128)} fusion(s32[32768]{0:T(1024)S(1)} %bitcast.9, bf16[32768,1024]{1,0:T(8,128)(2,1)} %bitcast.2, f32[]{:T(128)} %constant.10.clone.1), kind=kCustom, calls=%fused_computation.1 | custom fusion | flops 67108864 | bytes 100007936 | tf_op jit(solution)/shard_map/scatter-add | solution.py:28
  291.6 0.1 reduce-scatter.2.cloned.1.call-update
  292.9 167.7 %reduce-scatter.2.cloned.1.call-done = f32[8032,128]{1,0:T(8,128)} async-done(((f32[8032,1024]{1,0:T(8,128)}), f32[8032,128]{1,0:T(8,128)}) %reduce-scatter.2.cloned.1.call-update) | async-done | bytes 4112400 | tf_op jit(solution)/shard_map/reduce_scatter | solution.py:29
  460.6 13.3 %fusion.3 = (bf16[8032,128]{1,0:T(8,128)(2,1)}, f32[8032,128]{1,0:T(8,128)}, f32[8032,128]{1,0:T(8,128)}, f32[8032,128]{1,0:T(8,128)}) fusion(f32[8032,128]{1,0:T(8,128)} %param.11, f32[]{:T(128)S(6)} %mul.65, f32[]{:T(128)S(6)} %copy.13, f32[8032,128]{1,0:T(8,128)} %reduce-scatter.2.cloned.1.call-done, f32[8032,128]{1,0:T(8,128)} %param.10, f32[]{:T(128)S(6)} %copy.14, ...), kind=kLoop, calls=%fused_computation.10 | loop fusion | flops 16449536 | bytes 34955276 | tf_op jit(solution)/shard_map/convert_element_type | solution.py:15
Async XLA Ops:
  7.2 453.4 %reduce-scatter.2.cloned.1.call-start = ((), (), s32[]{:S(2)}) async-start(), calls=%async_computation.1 | async-start | bytes 37011456 | tf_op jit(solution)/shard_map/reduce_scatter | solution.py:29
Sparse Core Ops, SparseCore 0:
  291.7 168.8 reduce-scatter.1
where the time goes:
time: 481 us
  other arithmetic  297 us (62%)
  waiting for transfers between devices  168 us (35%)
  between operations  15.4 us (3%)
    scatter-add x1, other arithmetic, local_step(): jax.ops.segment_sum(out_grad.reshape(-1, model_dim).astype(jnp.float32),...  283 us
    reduce_scatter x1, waiting for transfers between devices, local_step(): lax.psum_scatter(dense_part, 'fsdp', scatter_dimension=1, tiled=True)  168 us
    convert_element_type x1, other arithmetic, adafactor_update(): return (new_w, new_m, new_v, new_w.astype(jnp.bfloat16))  13.3 us
  transfers between devices with their start and end apart: 1, of which 1 were waited for; matrix products, arithmetic and copies ran while one was open for 0% of the time, Pallas kernels for 0%

commit v1 on v0

v1 whole, which is shorter than its diff:
```python
import functools

import jax
import jax.numpy as jnp
from jax import lax
from jax.experimental import pallas as pl
from jax.experimental.pallas import tpu as pltpu
from jax.sharding import PartitionSpec as P

OPT_STEP = 20
LANES = 128
TILE = 256
GROUP = 16
CORES = 2
PIECES = 8
MESH = pl.DeviceIdType.MESH


def adafactor_update(embed_grad, head_grad, master_w, moment_m, moment_v, learn_rate, clip_scale):
    beta_two = 1.0 - OPT_STEP ** -0.8
    grad_full = clip_scale * (embed_grad + head_grad)
    new_v = beta_two * moment_v + (1.0 - beta_two) * (grad_full * grad_full + 1e-30)
    new_m = 0.9 * moment_m + 0.1 * (grad_full / jnp.sqrt(new_v))
    new_w = master_w - learn_rate * new_m - learn_rate * learn_rate * master_w
    return new_w, new_m, new_v, new_w.astype(jnp.bfloat16)


def unique_lists(tokens, n_class, rows):
    n_seq, seq_len = tokens.shape
    bits = int(rows).bit_length()
    me = lax.axis_index("tp")
    mine = tokens % n_class == me
    seq = lax.broadcasted_iota(jnp.int32, tokens.shape, 0)
    high = seq << (bits + 1)
    flag = 1 << bits
    key = jnp.where(mine, high + tokens // n_class, high + flag).reshape(-1)
    key = lax.sort(key)
    previous = jnp.concatenate([jnp.full((1,), -1, key.dtype), key[:-1]])
    padding = (key >> (bits + 1) << (bits + 1)) + flag
    key = lax.sort(jnp.where(key == previous, padding, key))
    slots = (key & (2 * flag - 1)).reshape(n_seq, seq_len)
    valid = slots < flag
    counts = jnp.sum(valid.astype(jnp.int32), axis=1)
    full = jnp.where(valid, slots * n_class + me, -1)
    return jnp.where(valid, slots, rows), full, counts


def scatter_kernel(rows, pitch, slot_ref, count_ref, tok_ref, full_ref, x_ref, out_ref, acc, onehot, sums, sem):
    b = pl.program_id(0)
    blocks = x_ref.shape[2] // LANES
    seq_len = x_ref.shape[1]
    sum_pitch = sums.shape[0] // blocks

    @pl.when(b == 0)
    def _():
        step = 8 * 67 if acc.shape[0] % (8 * 67) == 0 else 8

        def zero(i, carry):
            acc[pl.ds(pl.multiple_of(i * step, 8), step), :] = jnp.zeros((step, LANES), jnp.float32)
            return carry

        lax.fori_loop(0, acc.shape[0] // step, zero, 0)

    count = count_ref[b]
    tok = tok_ref[0]

    def tile(k, carry):
        row = full_ref[0, pl.ds(k, 1), :]
        eye = lax.broadcasted_iota(jnp.int32, (TILE, TILE), 0) == lax.broadcasted_iota(jnp.int32, (TILE, TILE), 1)
        col = jnp.sum(jnp.where(eye, row.astype(jnp.float32), 0.0), axis=1, keepdims=True).astype(jnp.int32)
        chunk = 512
        for j in range(0, seq_len, chunk):
            hit = col == tok[:, j : j + chunk]
            onehot[:, j : j + chunk] = jnp.where(hit, 1.0, 0.0).astype(jnp.bfloat16)
        for c in range(0, blocks, 2):
            part = jnp.dot(onehot[...], x_ref[0, :, c * LANES : (c + 2) * LANES], preferred_element_type=jnp.float32)
            sums[c * sum_pitch : c * sum_pitch + TILE, :] = part[:, :LANES]
            sums[(c + 1) * sum_pitch : (c + 1) * sum_pitch + TILE, :] = part[:, LANES:]

        left = jnp.minimum(count - k * TILE, TILE)

        def group(g, carry):
            base = b * seq_len + k * TILE + g * GROUP
            ids = [slot_ref[base + i] for i in range(GROUP)]
            old = [acc[pl.ds(v, blocks, stride=pitch), :] for v in ids]
            new = [a + sums[pl.ds(g * GROUP + i, blocks, stride=sum_pitch), :] for i, a in enumerate(old)]
            for v, a in zip(ids, new):
                acc[pl.ds(v, blocks, stride=pitch), :] = a
            return carry

        lax.fori_loop(0, (left + GROUP - 1) // GROUP, group, 0)
        return carry

    lax.fori_loop(0, (count + TILE - 1) // TILE, tile, 0)

    @pl.when(b == pl.num_programs(0) - 1)
    def _():
        copies = [
            pltpu.make_async_copy(acc.at[pl.ds(c * pitch, rows), :], out_ref.at[c], sem.at[c]) for c in range(blocks)
        ]
        for copy in copies:
            copy.start()
        for copy in copies:
            copy.wait()


def class_sums(tokens, out_grad, n_class, rows):
    n_seq, seq_len, width = out_grad.shape
    blocks = width // LANES
    pitch = rows + 8
    slots, full, counts = unique_lists(tokens, n_class, rows)
    return pl.pallas_call(
        functools.partial(scatter_kernel, rows, pitch),
        out_shape=jax.ShapeDtypeStruct((blocks, rows, LANES), jnp.float32),
        grid_spec=pltpu.PrefetchScalarGridSpec(
            num_scalar_prefetch=2,
            grid=(n_seq,),
            in_specs=[
                pl.BlockSpec((1, 1, seq_len), lambda b, *_: (b, 0, 0)),
                pl.BlockSpec((1, seq_len // TILE, TILE), lambda b, *_: (b, 0, 0)),
                pl.BlockSpec((1, seq_len, width), lambda b, *_: (b, 0, 0)),
            ],
            out_specs=pl.BlockSpec(memory_space=pl.ANY),
            scratch_shapes=[
                pltpu.VMEM((blocks * pitch, LANES), jnp.float32),
                pltpu.VMEM((TILE, seq_len), jnp.bfloat16),
                pltpu.VMEM((blocks * (TILE + 8), LANES), jnp.float32),
                pltpu.SemaphoreType.DMA((blocks,)),
            ],
        ),
        compiler_params=pltpu.CompilerParams(vmem_limit_bytes=60 * 1024 * 1024, dimension_semantics=("arbitrary",)),
        name="class_sums",
    )(slots.reshape(-1), counts, tokens.reshape(n_seq, 1, seq_len), full.reshape(n_seq, seq_len // TILE, TILE), out_grad)


def split_rows(rows, pieces):
    tiles = rows // 8
    sizes = [tiles // (2 * pieces) + (i < tiles % (2 * pieces)) for i in range(2 * pieces)]
    starts = [8 * sum(sizes[:i]) for i in range(2 * pieces)]
    spans = [(s, 8 * n) for s, n in zip(starts, sizes)]
    return spans[0::2], spans[1::2]


def exchange_kernel(n_x, n_tp, spans, part, out, own, sib, rec, got, load_sem, sib_sem, ring_sem, y_sem):
    pos = lax.axis_index("fsdp")
    me_y = lax.axis_index("tp")
    core = lax.rem(pos, CORES)
    me_x = pos // CORES
    other = 1 - core

    def at_x(x):
        return {"fsdp": lax.rem(x + n_x, n_x) * CORES + core}

    def at_y(d):
        return {"tp": lax.rem(me_y + d, n_tp)}

    sibling = {"fsdp": me_x * CORES + other}
    sides = [at_x(me_x + 1), at_x(me_x + n_x - 1)]

    barrier = pltpu.get_barrier_semaphore()
    peers = [sibling] + sides + [at_y(d) for d in range(1, n_tp)]
    for peer in peers:
        pl.semaphore_signal(barrier, inc=1, device_id=peer, device_id_type=MESH)
    pl.semaphore_wait(barrier, len(peers))

    def load(p, d):
        s, n = spans[d][p]
        return pltpu.make_async_copy(part.at[:, core, :, pl.ds(s, n), :], own.at[:, :, pl.ds(s, n), :], load_sem.at[d, p])

    def to_sibling(p, d):
        s, n = spans[d][p]
        return pltpu.make_async_remote_copy(
            src_ref=part.at[:, other, :, pl.ds(s, n), :],
            dst_ref=sib.at[:, :, pl.ds(s, n), :],
            send_sem=sib_sem.at[0, d, p],
            recv_sem=sib_sem.at[1, d, p],
            device_id=sibling,
            device_id_type=MESH,
        )

    def owner(d, step):
        return lax.rem(me_x + n_x - step, n_x) if d == 0 else lax.rem(me_x + step, n_x)

    def hop(p, d, step):
        s, n = spans[d][p]
        return pltpu.make_async_remote_copy(
            src_ref=own.at[owner(d, step), :, pl.ds(s, n), :],
            dst_ref=rec.at[step - 1, :, pl.ds(s, n), :],
            send_sem=ring_sem.at[0, d, step - 1, p],
            recv_sem=ring_sem.at[1, d, step - 1, p],
            device_id=sides[d],
            device_id_type=MESH,
        )

    def to_row(p, d, k):
        s, n = spans[d][p]
        return pltpu.make_async_remote_copy(
            src_ref=own.at[me_x, lax.rem(me_y + k, n_tp), pl.ds(s, n), :],
            dst_ref=got.at[k - 1, pl.ds(s, n), :],
            send_sem=y_sem.at[0, d, k - 1, p],
            recv_sem=y_sem.at[1, d, k - 1, p],
            device_id=at_y(k),
            device_id_type=MESH,
        )

    def add(p, d, step):
        s, n = spans[d][p]
        x = owner(d, step)
        for y in range(n_tp):
            total = own[x, y, pl.ds(s, n), :] + sib[x, y, pl.ds(s, n), :]
            if step > 1:
                total = total + rec[step - 2, y, pl.ds(s, n), :]
            own[x, y, pl.ds(s, n), :] = total

    pieces = len(spans[0])
    for p in range(pieces):
        for d in range(2):
            load(p, d).start()
            to_sibling(p, d).start()

    for t in range(pieces + n_x - 1):
        for step in range(1, n_x + 1):
            p = t - step + 1
            if not 0 <= p < pieces:
                continue
            for d in range(2):
                if step == 1:
                    load(p, d).wait()
                    to_sibling(p, d).wait_recv()
                else:
                    hop(p, d, step - 1).wait_recv()
                add(p, d, step)
                if step < n_x:
                    hop(p, d, step).start()
                else:
                    for k in range(1, n_tp):
                        to_row(p, d, k).start()

    for p in range(pieces):
        for d in range(2):
            s, n = spans[d][p]
            out[pl.ds(s * n_tp + me_y, n, stride=n_tp), :] = own[me_x, me_y, pl.ds(s, n), :]
            for k in range(1, n_tp):
                to_row(p, d, k).wait_recv()
                source = lax.rem(me_y + n_tp - k, n_tp)
                out[pl.ds(s * n_tp + source, n, stride=n_tp), :] = got[k - 1, pl.ds(s, n), :]

    for p in range(pieces):
        for d in range(2):
            to_sibling(p, d).wait_send()
            for step in range(1, n_x):
                hop(p, d, step).wait_send()
            for k in range(1, n_tp):
                to_row(p, d, k).wait_send()


def reduce_and_place(part, n_x, n_tp, rows):
    sub = rows // n_tp
    spans = split_rows(sub, PIECES)
    full = (n_x, n_tp, sub, LANES)
    return pl.pallas_call(
        functools.partial(exchange_kernel, n_x, n_tp, spans),
        out_shape=jax.ShapeDtypeStruct((rows, LANES), jnp.float32),
        in_specs=[pl.BlockSpec(memory_space=pl.ANY)],
        out_specs=pl.BlockSpec(memory_space=pltpu.VMEM),
        scratch_shapes=[
            pltpu.VMEM(full, jnp.float32),
            pltpu.VMEM(full, jnp.float32),
            pltpu.VMEM((n_x - 1, n_tp, sub, LANES), jnp.float32),
            pltpu.VMEM((n_tp - 1, sub, LANES), jnp.float32),
            pltpu.SemaphoreType.DMA((2, PIECES)),
            pltpu.SemaphoreType.DMA((2, 2, PIECES)),
            pltpu.SemaphoreType.DMA((2, 2, n_x - 1, PIECES)),
            pltpu.SemaphoreType.DMA((2, 2, n_tp - 1, PIECES)),
        ],
        compiler_params=pltpu.CompilerParams(
            collective_id=0, has_side_effects=True, vmem_limit_bytes=62 * 1024 * 1024
        ),
        name="reduce_and_place",
    )(part.reshape(n_x, CORES, n_tp, sub, LANES))


def solution(mesh):
    row_spec = P(("dp", "fsdp"), None)
    act_spec = P(("dp", "fsdp"), None, None)
    table_spec = P(("dp", "tp"), "fsdp")
    n_tp = mesh.shape["tp"]
    n_x = mesh.shape["fsdp"] // CORES

    def local_step(tokens, out_grad, head_grad, master_w, moment_m, moment_v, learn_rate, clip_scale):
        rows = master_w.shape[0]
        part = class_sums(tokens, out_grad, n_tp, rows)
        embed_grad = reduce_and_place(part, n_x, n_tp, rows)
        return adafactor_update(embed_grad, head_grad, master_w, moment_m, moment_v, learn_rate, clip_scale)

    return jax.shard_map(local_step, mesh=mesh, in_specs=(row_spec, act_spec, table_spec, table_spec, table_spec, table_spec, P(), P()), out_specs=(table_spec, table_spec, table_spec, table_spec), check_vma=False)
```

time: 481 us -> 252 us (0.52)
  other arithmetic: 297 us -> 38.3 us
  Pallas kernels: 0 us -> 209 us
  waiting for transfers between devices: 168 us -> 0 us
  between operations: 15.4 us -> 2 us
    scatter-add x1 -> x0, other arithmetic: 283 us -> none  [local_step(): jax.ops.segment_sum(out_grad.reshape(-1, model_dim).astype(jnp.float32),...]
    pallas_call x0 -> x2, Pallas kernels: none -> 209 us  [the longest x1 158 us: reduce_and_place(): pl.pallas_call(functools.partial(exchange_kernel, n_x, n_tp, spans), out_...]
    reduce_scatter x1 -> x0, waiting for transfers between devices: 168 us -> none  [local_step(): lax.psum_scatter(dense_part, 'fsdp', scatter_dimension=1, tiled=True)]
    sort x0 -> x2, other arithmetic: none -> 22.5 us  [the longest x1 11.3 us: unique_lists(): key = lax.sort(jnp.where(key == previous, padding, key))]
  transfers between devices with their start and end apart: 1 -> 0, of which waited for: 1 -> 0; matrix products, arithmetic and copies ran while one was open for 0% -> 0% of each run, Pallas kernels for 0% -> 0%
where the time goes in v1:
time: 252 us
  Pallas kernels  209 us (83%)
  other arithmetic  38.3 us (15%)
    pallas_call x1, Pallas kernels, reduce_and_place(): pl.pallas_call(functools.partial(exchange_kernel, n_x, n_tp, spans), out_...  158 us
    pallas_call x1, Pallas kernels, class_sums(): pl.pallas_call(functools.partial(scatter_kernel, rows, pitch), out_shape=...  51.3 us
    convert_element_type x1, other arithmetic, adafactor_update(): return (new_w, new_m, new_v, new_w.astype(jnp.bfloat16))  13.3 us
    sort x1, other arithmetic, unique_lists(): key = lax.sort(jnp.where(key == previous, padding, key))  11.3 us
    sort x1, other arithmetic, unique_lists(): key = lax.sort(key)  11.2 us

profile of v1, /device:TPU:97, one launch (start us, length us, event | category | flops | bytes accessed | tf_op | source)
XLA Modules:
  0.0 251.7 jit_solution(18227869842338488536)
XLA Ops:
  0.6 1.0 fusion.3
  1.7 11.2 %sort.28 = (s32[32768]{0:T(1024)S(1)}, s32[32768]{0:T(1024)}) sort(s32[32768]{0:T(1024)S(1)} %bitcast.7, s32[32768]{0:T(1024)S(1)} %iota.19), dimensions={0}, to_apply=%region_0.1 | sort | flops 491520 | bytes 524288 | tf_op jit(solution)/shard_map/sort | solution.py:37
  12.9 0.1 compare_select_fusion
  13.0 11.3 %sort.29 = (s32[32768]{0:T(1024)S(1)}, s32[32768]{0:T(1024)}) sort(s32[32768]{0:T(1024)S(1)} %compare_select_fusion, s32[32768]{0:T(1024)S(1)} %iota.20), dimensions={0}, to_apply=%region_1.2 | sort | flops 491520 | bytes 524288 | tf_op jit(solution)/shard_map/sort | solution.py:40
  24.4 0.7 add_select_fusion.2
  25.1 0.7 select_n.37.full_ref
  25.8 0.6 reduce_sum.9.count_ref
  26.4 1.6 reshape.34.tok_ref
  28.1 51.3 %class_sums.1 = f32[8,8032,128]{2,1,0:T(8,128)} custom-call(s32[32768]{0:T(1024)} %get-tuple-element.15.slot_ref, s32[16]{0:T(128)} %reduce_sum.9.count_ref, s32[16,1,2048]{2,1,0:T(1,128)} %reshape.34.tok_ref, s32[16,8,256]{2,1,0:T(8,128)} %select_n.37.full_ref, bf16[16,2048,1024]{2,1,0:T(8,128)(2,1)} %x_ref.1), custom_call_target="tpu_custom_call" | custom-call | tf_op jit(solution)/shard_map/class_sums/pallas_call | solution.py:112
  79.4 157.6 %reduce_and_place.1 = f32[8032,128]{1,0:T(8,128)} custom-call(f32[4,2,4,2008,128]{4,3,2,1,0:T(8,128)} %bitcast.5), custom_call_target="tpu_custom_call" | custom-call | tf_op jit(solution)/shard_map/reduce_and_place/pallas_call | solution.py:261
  238.4 13.3 %fusion.7 = (bf16[8032,128]{1,0:T(8,128)(2,1)}, f32[8032,128]{1,0:T(8,128)}, f32[8032,128]{1,0:T(8,128)}, f32[8032,128]{1,0:T(8,128)}) fusion(f32[8032,128]{1,0:T(8,128)} %param.11, f32[]{:T(128)S(6)} %mul.68, f32[]{:T(128)S(6)} %copy.13, f32[8032,128]{1,0:T(8,128)} %reduce_and_place.1, f32[8032,128]{1,0:T(8,128)} %param.10, f32[]{:T(128)S(6)} %copy.14, ...), kind=kLoop, calls=%fused_computation.23 | loop fusion | flops 16449536 | bytes 34955276 | tf_op jit(solution)/shard_map/convert_element_type | solution.py:25
  (6 shorter events, 0.1 us)

commit v2 on v1

--- a/solution.py
+++ b/solution.py
@@ -2,6 +2,7 @@
 
 import jax
 import jax.numpy as jnp
+import numpy as np
 from jax import lax
 from jax.experimental import pallas as pl
 from jax.experimental.pallas import tpu as pltpu
@@ -12,8 +13,22 @@
 TILE = 256
 GROUP = 16
 CORES = 2
-PIECES = 8
+PIECES = 2
+CHUNKS = 8
+CAPACITY = 272
+SLOT_BITS = 9
+FIRST, DIRECT, SECOND = 4, 2, 1
 MESH = pl.DeviceIdType.MESH
+
+
+def bits(power):
+    return int(power).bit_length() - 1
+
+
+def layout(rows, n_tp):
+    sub = rows // n_tp
+    span = pl.next_power_of_2(pl.cdiv(sub, CHUNKS))
+    return sub, span, span * n_tp, span * n_tp * CHUNKS
 
 
 def adafactor_update(embed_grad, head_grad, master_w, moment_m, moment_v, learn_rate, clip_scale):
@@ -25,70 +40,85 @@
     return new_w, new_m, new_v, new_w.astype(jnp.bfloat16)
 
 
-def unique_lists(tokens, n_class, rows):
-    n_seq, seq_len = tokens.shape
-    bits = int(rows).bit_length()
-    me = lax.axis_index("tp")
-    mine = tokens % n_class == me
-    seq = lax.broadcasted_iota(jnp.int32, tokens.shape, 0)
-    high = seq << (bits + 1)
-    flag = 1 << bits
-    key = jnp.where(mine, high + tokens // n_class, high + flag).reshape(-1)
-    key = lax.sort(key)
-    previous = jnp.concatenate([jnp.full((1,), -1, key.dtype), key[:-1]])
-    padding = (key >> (bits + 1) << (bits + 1)) + flag
-    key = lax.sort(jnp.where(key == previous, padding, key))
-    slots = (key & (2 * flag - 1)).reshape(n_seq, seq_len)
-    valid = slots < flag
-    counts = jnp.sum(valid.astype(jnp.int32), axis=1)
-    full = jnp.where(valid, slots * n_class + me, -1)
-    return jnp.where(valid, slots, rows), full, counts
-
-
-def scatter_kernel(rows, pitch, slot_ref, count_ref, tok_ref, full_ref, x_ref, out_ref, acc, onehot, sums, sem):
+def count_of(key_ref, base, seq_len, pad):
+    count = jnp.int32(0)
+    half = seq_len // 2
+    while half:
+        count = jnp.where(key_ref[base + count + half - 1] & pad == 0, count + half, count)
+        half //= 2
+    return jnp.where(key_ref[base + count] & pad == 0, count + 1, count)
+
+
+def tile_sums(rows, n_tp, key, tok, x_ref, onehot, sums):
+    sub, span, chunk, size = layout(rows, n_tp)
+    seq_len, width = x_ref.shape[1:]
+    sum_pitch = sums.shape[0] // (width // LANES)
+    place = key >> SLOT_BITS & (size - 1)
+    row = ((place & (chunk - 1)) >> bits(span)) * sub + (place & (span - 1)) * CHUNKS + (place >> bits(chunk))
+    ids = jnp.where(key & size << SLOT_BITS == 0, row * n_tp + lax.axis_index("tp"), -1)
+    eye = lax.broadcasted_iota(jnp.int32, (TILE, TILE), 0) == lax.broadcasted_iota(jnp.int32, (TILE, TILE), 1)
+    col = jnp.sum(jnp.where(eye, ids.astype(jnp.float32), 0.0), axis=1, keepdims=True).astype(jnp.int32)
+    step = 512
+    for j in range(0, seq_len, step):
+        hit = col == tok[:, j : j + step]
+        onehot[:, j : j + step] = jnp.where(hit, 1.0, 0.0).astype(jnp.bfloat16)
+    for c in range(0, width // LANES, 2):
+        part = jnp.dot(onehot[...], x_ref[0, :, c * LANES : (c + 2) * LANES], preferred_element_type=jnp.float32)
+        sums[c * sum_pitch : c * sum_pitch + TILE, :] = part[:, :LANES]
+        sums[(c + 1) * sum_pitch : (c + 1) * sum_pitch + TILE, :] = part[:, LANES:]
+
+
+def clear(acc):
+    step = 8 * 28
+
+    def zero(i, carry):
+        acc[pl.ds(pl.multiple_of(i * step, 8), step), :] = jnp.zeros((step, LANES), jnp.float32)
+        return carry
+
+    lax.fori_loop(0, acc.shape[0] // step, zero, 0)
+    rest = acc.shape[0] % step
+    if rest:
+        acc[acc.shape[0] - rest :, :] = jnp.zeros((rest, LANES), jnp.float32)
+
+
+def add_rows(acc, sums, g, addresses):
+    blocks = 8
+    pitch, sum_pitch = acc.shape[0] // blocks, sums.shape[0] // blocks
+    old = [acc[pl.ds(a, blocks, stride=pitch), :] for a in addresses]
+    new = [o + sums[pl.ds(g * GROUP + i, blocks, stride=sum_pitch), :] for i, o in enumerate(old)]
+    for a, v in zip(addresses, new):
+        acc[pl.ds(a, blocks, stride=pitch), :] = v
+
+
+def scatter_kernel(rows, n_tp, key_ref, tok_ref, list_ref, x_ref, out_ref, acc, onehot, sums, sem):
     b = pl.program_id(0)
-    blocks = x_ref.shape[2] // LANES
-    seq_len = x_ref.shape[1]
-    sum_pitch = sums.shape[0] // blocks
+    seq_len, width = x_ref.shape[1:]
+    blocks = width // LANES
+    pitch = acc.shape[0] // blocks
+    sub, span, chunk, size = layout(rows, n_tp)
+    base = b * seq_len
 
     @pl.when(b == 0)
     def _():
-        step = 8 * 67 if acc.shape[0] % (8 * 67) == 0 else 8
-
-        def zero(i, carry):
-            acc[pl.ds(pl.multiple_of(i * step, 8), step), :] = jnp.zeros((step, LANES), jnp.float32)
+        clear(acc)
+
+    count = count_of(key_ref, base, seq_len, size << SLOT_BITS)
+    tok = tok_ref[pl.ds(b, 1), :]
+
+    def tile(k, carry):
+        tile_sums(rows, n_tp, list_ref[0, pl.ds(k, 1), :], tok, x_ref, onehot, sums)
+
+        def group(g, carry):
+            first = base + k * TILE + g * GROUP
+            addresses = []
+            for i in range(GROUP):
+                place = key_ref[first + i] >> SLOT_BITS & (2 * size - 1)
+                row = ((place & (chunk - 1)) >> bits(span)) * sub + (place & (span - 1)) * CHUNKS + (place >> bits(chunk))
+                addresses.append(jnp.where(place < size, row, rows))
+            add_rows(acc, sums, g, addresses)
             return carry
 
-        lax.fori_loop(0, acc.shape[0] // step, zero, 0)
-
-    count = count_ref[b]
-    tok = tok_ref[0]
-
-    def tile(k, carry):
-        row = full_ref[0, pl.ds(k, 1), :]
-        eye = lax.broadcasted_iota(jnp.int32, (TILE, TILE), 0) == lax.broadcasted_iota(jnp.int32, (TILE, TILE), 1)
-        col = jnp.sum(jnp.where(eye, row.astype(jnp.float32), 0.0), axis=1, keepdims=True).astype(jnp.int32)
-        chunk = 512
-        for j in range(0, seq_len, chunk):
-            hit = col == tok[:, j : j + chunk]
-            onehot[:, j : j + chunk] = jnp.where(hit, 1.0, 0.0).astype(jnp.bfloat16)
-        for c in range(0, blocks, 2):
-            part = jnp.dot(onehot[...], x_ref[0, :, c * LANES : (c + 2) * LANES], preferred_element_type=jnp.float32)
-            sums[c * sum_pitch : c * sum_pitch + TILE, :] = part[:, :LANES]
-            sums[(c + 1) * sum_pitch : (c + 1) * sum_pitch + TILE, :] = part[:, LANES:]
-
-        left = jnp.minimum(count - k * TILE, TILE)
-
-        def group(g, carry):
-            base = b * seq_len + k * TILE + g * GROUP
-            ids = [slot_ref[base + i] for i in range(GROUP)]
-            old = [acc[pl.ds(v, blocks, stride=pitch), :] for v in ids]
-            new = [a + sums[pl.ds(g * GROUP + i, blocks, stride=sum_pitch), :] for i, a in enumerate(old)]
-            for v, a in zip(ids, new):
-                acc[pl.ds(v, blocks, stride=pitch), :] = a
-            return carry
-
-        lax.fori_loop(0, (left + GROUP - 1) // GROUP, group, 0)
+        lax.fori_loop(0, (jnp.minimum(count - k * TILE, TILE) + GROUP - 1) // GROUP, group, 0)
         return carry
 
     lax.fori_loop(0, (count + TILE - 1) // TILE, tile, 0)
@@ -104,25 +134,23 @@
             copy.wait()
 
 
-def class_sums(tokens, out_grad, n_class, rows):
+def class_sums(keys, tokens, out_grad, n_tp, rows):
     n_seq, seq_len, width = out_grad.shape
     blocks = width // LANES
-    pitch = rows + 8
-    slots, full, counts = unique_lists(tokens, n_class, rows)
     return pl.pallas_call(
-        functools.partial(scatter_kernel, rows, pitch),
+        functools.partial(scatter_kernel, rows, n_tp),
         out_shape=jax.ShapeDtypeStruct((blocks, rows, LANES), jnp.float32),
         grid_spec=pltpu.PrefetchScalarGridSpec(
-            num_scalar_prefetch=2,
+            num_scalar_prefetch=1,
             grid=(n_seq,),
             in_specs=[
-                pl.BlockSpec((1, 1, seq_len), lambda b, *_: (b, 0, 0)),
+                pl.BlockSpec((n_seq, seq_len), lambda b, *_: (0, 0)),
                 pl.BlockSpec((1, seq_len // TILE, TILE), lambda b, *_: (b, 0, 0)),
                 pl.BlockSpec((1, seq_len, width), lambda b, *_: (b, 0, 0)),
             ],
             out_specs=pl.BlockSpec(memory_space=pl.ANY),
             scratch_shapes=[
-                pltpu.VMEM((blocks * pitch, LANES), jnp.float32),
+                pltpu.VMEM((blocks * (rows + 8), LANES), jnp.float32),
                 pltpu.VMEM((TILE, seq_len), jnp.bfloat16),
                 pltpu.VMEM((blocks * (TILE + 8), LANES), jnp.float32),
                 pltpu.SemaphoreType.DMA((blocks,)),
@@ -130,7 +158,7 @@
         ),
         compiler_params=pltpu.CompilerParams(vmem_limit_bytes=60 * 1024 * 1024, dimension_semantics=("arbitrary",)),
         name="class_sums",
-    )(slots.reshape(-1), counts, tokens.reshape(n_seq, 1, seq_len), full.reshape(n_seq, seq_len // TILE, TILE), out_grad)
+    )(keys, tokens, keys.reshape(n_seq, seq_len // TILE, TILE), out_grad)
 
 
 def split_rows(rows, pieces):
@@ -280,6 +308,344 @@
     )(part.reshape(n_x, CORES, n_tp, sub, LANES))
 
 
+def slot_kernel(size, chunk, n_seq, s_ref, key_ref, over_ref):
+    s = s_ref[...]
+    height, absent = s.shape[0], CAPACITY - 1
+    row = lax.broadcasted_iota(jnp.int32, s.shape, 0)
+    lane = lax.broadcasted_iota(jnp.int32, s.shape, 1)
+    turned = pltpu.roll(s, 1, 1)
+    previous = jnp.where(lane == 0, pltpu.roll(turned, 1, 0), turned)
+    previous = jnp.where((lane == 0) & (row == 0), -1, previous)
+    place = s >> bits(n_seq)
+    fresh = ((place != previous >> bits(n_seq)) & (place < size)).astype(jnp.float32)
+    upto = lax.broadcasted_iota(jnp.int32, (LANES, LANES), 0) <= lax.broadcasted_iota(jnp.int32, (LANES, LANES), 1)
+    inner = jnp.dot(fresh.astype(jnp.bfloat16), upto.astype(jnp.float32).astype(jnp.bfloat16), preferred_element_type=jnp.float32)
+    total = jnp.broadcast_to(inner[:, LANES - 1 :], s.shape).astype(jnp.bfloat16)
+    above = lax.broadcasted_iota(jnp.int32, (height, height), 1) < lax.broadcasted_iota(jnp.int32, (height, height), 0)
+    outer = jnp.dot(above.astype(jnp.float32).astype(jnp.bfloat16), total, preferred_element_type=jnp.float32)
+    rank = (inner + outer).astype(jnp.int32) - 1
+    part = place >> bits(chunk)
+    ends = [jnp.sum(jnp.where(part <= q, fresh, 0.0)).astype(jnp.int32) for q in range(CHUNKS)]
+    start = jnp.zeros_like(s)
+    over = (ends[0] > absent).astype(jnp.int32)
+    for q in range(1, CHUNKS):
+        start = jnp.where(part == q, ends[q - 1], start)
+        over = jnp.maximum(over, (ends[q] - ends[q - 1] > absent).astype(jnp.int32))
+    slot = jnp.minimum(rank - start, absent)
+    padding = (s == previous) | (place >= size)
+    low = jnp.where(padding, size << SLOT_BITS, (place << SLOT_BITS) + slot)
+    key_ref[...] = (s & (n_seq - 1)) * (2 * size << SLOT_BITS) + low
+    over_ref[0] = over
+
+
+def sorted_keys(tokens, n_tp, rows):
+    n_seq, seq_len = tokens.shape
+    sub, span, chunk, size = layout(rows, n_tp)
+    row = tokens // n_tp
+    inner = row % sub
+    place = inner % CHUNKS * chunk + row // sub * span + inner // CHUNKS
+    place = jnp.where(tokens % n_tp == lax.axis_index("tp"), place, size)
+    key = lax.sort((place * n_seq + lax.broadcasted_iota(jnp.int32, tokens.shape, 0)).reshape(-1))
+    key, over = pl.pallas_call(
+        functools.partial(slot_kernel, size, chunk, n_seq),
+        out_shape=(jax.ShapeDtypeStruct((key.shape[0] // LANES, LANES), jnp.int32), jax.ShapeDtypeStruct((1,), jnp.int32)),
+        out_specs=(pl.BlockSpec(memory_space=pltpu.VMEM), pl.BlockSpec(memory_space=pltpu.SMEM)),
+        name="slots",
+    )(key.reshape(-1, LANES))
+    return lax.sort(key.reshape(-1)), over
+
+
+def compact_kernel(rows, n_tp, key_ref, over_ref, tok_ref, list_ref, x_ref, empty_ref, out_ref, table_ref, acc, onehot, sums, table, sem):
+    b = pl.program_id(0)
+    seq_len, width = x_ref.shape[1:]
+    blocks = width // LANES
+    pitch = acc.shape[0] // blocks
+    sub, span, chunk, size = layout(rows, n_tp)
+    base = b * seq_len
+
+    @pl.when(b == 0)
+    def _():
+        fill = pltpu.make_async_copy(empty_ref, table, sem.at[0])
+        fill.start()
+        clear(acc)
+        fill.wait()
+
+    count = count_of(key_ref, base, seq_len, size << SLOT_BITS)
+    tok = tok_ref[pl.ds(b, 1), :]
+
+    def tile(k, carry):
+        tile_sums(rows, n_tp, list_ref[0, pl.ds(k, 1), :], tok, x_ref, onehot, sums)
+
+        def group(g, carry):
+            first = base + k * TILE + g * GROUP
+            addresses = []
+            for i in range(GROUP):
+                key = key_ref[first + i]
+                slot = key & ((1 << SLOT_BITS) - 1)
+                place = key >> SLOT_BITS & (2 * size - 1)
+                table[place] = slot
+                addresses.append((place >> bits(chunk)) * CAPACITY + slot)
+            add_rows(acc, sums, g, addresses)
+            return carry
+
+        lax.fori_loop(0, (jnp.minimum(count - k * TILE, TILE) + GROUP - 1) // GROUP, group, 0)
+        return carry
+
+    lax.fori_loop(0, (count + TILE - 1) // TILE, tile, 0)
+
+    @pl.when(b == pl.num_programs(0) - 1)
+    def _():
+        table[span - 1] = over_ref[0]
+        copies = [
+            pltpu.make_async_copy(acc.at[pl.ds(c * pitch, CHUNKS * CAPACITY), :], out_ref.at[c], sem.at[c + 1])
+            for c in range(blocks)
+        ]
+        copies.append(pltpu.make_async_copy(table.at[pl.ds(0, size)], table_ref, sem.at[0]))
+        for copy in copies:
+            copy.start()
+        for copy in copies:
+            copy.wait()
+
+
+def compact_sums(keys, over, tokens, out_grad, n_tp, rows):
+    n_seq, seq_len, width = out_grad.shape
+    blocks = width // LANES
+    _, span, chunk, size = layout(rows, n_tp)
+    empty = np.full((size + chunk,), CAPACITY - 1, np.int32)
+    empty[size:] = 0
+    empty[span - 1] = 0
+    return pl.pallas_call(
+        functools.partial(compact_kernel, rows, n_tp),
+        out_shape=(
+            jax.ShapeDtypeStruct((blocks, CHUNKS * CAPACITY, LANES), jnp.float32),
+            jax.ShapeDtypeStruct((size,), jnp.int32),
+        ),
+        grid_spec=pltpu.PrefetchScalarGridSpec(
+            num_scalar_prefetch=2,
+            grid=(n_seq,),
+            in_specs=[
+                pl.BlockSpec((n_seq, seq_len), lambda b, *_: (0, 0)),
+                pl.BlockSpec((1, seq_len // TILE, TILE), lambda b, *_: (b, 0, 0)),
+                pl.BlockSpec((1, seq_len, width), lambda b, *_: (b, 0, 0)),
+                pl.BlockSpec(memory_space=pl.ANY),
+            ],
+            out_specs=(pl.BlockSpec(memory_space=pl.ANY), pl.BlockSpec(memory_space=pl.ANY)),
+            scratch_shapes=[
+                pltpu.VMEM((blocks * (CHUNKS * CAPACITY + 8), LANES), jnp.float32),
+                pltpu.VMEM((TILE, seq_len), jnp.bfloat16),
+                pltpu.VMEM((blocks * (TILE + 8), LANES), jnp.float32),
+                pltpu.SMEM((size + chunk,), jnp.int32),
+                pltpu.SemaphoreType.DMA((blocks + 1,)),
+            ],
+        ),
+        compiler_params=pltpu.CompilerParams(vmem_limit_bytes=40 * 1024 * 1024, dimension_semantics=("arbitrary",)),
+        name="compact_sums",
+    )(keys, over, tokens, keys.reshape(n_seq, seq_len // TILE, TILE), out_grad, jnp.asarray(empty))
+
+
+def star_kernel(rows, n_x, n_tp, comp, table, out, tables, *scratch):
+    rec = scratch[:CHUNKS]
+    transit, dense, got, lookup, table_sem, direct_sem, rec_sem, transit_sem, forward_sem, y_sem = scratch[CHUNKS:]
+    sub, span, chunk, size = layout(rows, n_tp)
+    n_f = n_x * CORES
+    pos = lax.axis_index("fsdp")
+    me_y = lax.axis_index("tp")
+    core = lax.rem(pos, CORES)
+    me_x = pos // CORES
+
+    def at(dx, c):
+        return lax.rem(me_x + n_x + dx, n_x) * CORES + c
+
+    near = [at(0, 1 - core), at(1, 0), at(1, 1), at(-1, 0), at(-1, 1)]
+    others = [lax.rem(pos + k, n_f) for k in range(1, n_f)]
+
+    def at_y(d):
+        return {"tp": lax.rem(me_y + d, n_tp)}
+
+    barrier = pltpu.get_barrier_semaphore()
+    peers = [{"fsdp": f} for f in others] + [at_y(d) for d in range(1, n_tp)]
+    for peer in peers:
+        pl.semaphore_signal(barrier, inc=1, device_id=peer, device_id_type=MESH)
+    pl.semaphore_wait(barrier, len(peers))
+
+    def remote(src, dst, send, recv, device):
+        return pltpu.make_async_remote_copy(
+            src_ref=src, dst_ref=dst, send_sem=send, recv_sem=recv, device_id=device, device_id_type=MESH
+        )
+
+    def rows_of(dest, q):
+        return comp.at[dest, pl.ds(q * CAPACITY, CAPACITY), :]
+
+    def direct(q, j):
+        return remote(rows_of(near[j], q), rec[q].at[pos], direct_sem.at[q, j], rec_sem.at[q, pos], {"fsdp": near[j]})
+
+    def stay(q):
+        return pltpu.make_async_copy(rows_of(pos, q), rec[q].at[pos], rec_sem.at[q, pos])
+
+    def turn(q):
+        return 1 if q % 2 == 0 else -1
+
+    def first_leg(q, c):
+        return remote(
+            rows_of(at(2, c), q), transit.at[q, c], transit_sem.at[0, q, c], transit_sem.at[1, q, c], {"fsdp": at(turn(q), core)}
+        )
+
+    def second_leg(q, c):
+        origin = at(-turn(q), core)
+        return remote(
+            transit.at[q, c], rec[q].at[origin], forward_sem.at[q, c], rec_sem.at[q, origin], {"fsdp": at(turn(q), c)}
+        )
+
+    def arrival(q, f):
+        return remote(rec[q].at[f], rec[q].at[f], direct_sem.at[q, 0], rec_sem.at[q, f], {"fsdp": near[0]})
+
+    def table_to(k):
+        mine = tables.at[pl.ds(pos * size, size)]
+        return remote(table, mine, table_sem.at[0, k], table_sem.at[1, pos], {"fsdp": others[k]})
+
+    def table_from(k):
+        theirs = tables.at[pl.ds(others[k] * size, size)]
+        return remote(table, theirs, table_sem.at[0, k], table_sem.at[1, others[k]], {"fsdp": others[k]})
+
+    def to_row(q, k):
+        return remote(
+            dense.at[q, pl.ds(lax.rem(me_y + k, n_tp) * span, span), :], got.at[q, k - 1], y_sem.at[0, q, k - 1], y_sem.at[1, q, k - 1], at_y(k)
+        )
+
+    def start_first(q):
+        if q < CHUNKS:
+            for c in range(CORES):
+                first_leg(q, c).start()
+
+    def start_direct(q):
+        if q < CHUNKS:
+            for j in range(len(near)):
+                direct(q, j).start()
+            stay(q).start()
+
+    def start_second(q):
+        if q < CHUNKS:
+            for c in range(CORES):
+                first_leg(q, c).wait_recv()
+                second_leg(q, c).start()
+
+    for q in range(max(FIRST, DIRECT)):
+        if q < FIRST:
+            start_first(q)
+        if q < DIRECT:
+            start_direct(q)
+        if q == 0:
+            for k in range(n_f - 1):
+                table_to(k).start()
+    own_table = pltpu.make_async_copy(table, lookup.at[pl.ds(pos * size, size)], table_sem.at[2, pos])
+    own_table.start()
+    for k in range(n_f - 1):
+        table_from(k).wait_recv()
+        f = others[k]
+        pltpu.make_async_copy(tables.at[pl.ds(f * size, size)], lookup.at[pl.ds(f * size, size)], table_sem.at[2, f]).start()
+    own_table.wait()
+    for k in range(n_f - 1):
+        f = others[k]
+        pltpu.make_async_copy(tables.at[pl.ds(f * size, size)], lookup.at[pl.ds(f * size, size)], table_sem.at[2, f]).wait()
+
+    def expand(q, y, n):
+        def eight(g, carry):
+            for i in range(8):
+                entry = q * chunk + y * span + g * 8 + i
+                total = rec[q][0, pl.ds(lookup[entry], 1), :]
+                for f in range(1, n_f):
+                    total = total + rec[q][f, pl.ds(lookup[f * size + entry], 1), :]
+                dense[q, pl.ds(y * span + g * 8 + i, 1), :] = total
+            return carry
+
+        lax.fori_loop(0, n * span // 8, eight, 0)
+
+    def mark(q, y):
+        over = lookup[span - 1]
+        for f in range(1, n_f):
+            over = over + lookup[f * size + span - 1]
+        dense[q, y * span + span - 1 : y * span + span, :] = jnp.full((1, LANES), over.astype(jnp.float32))
+
+    def place(q):
+        out[pl.ds(q * n_tp + me_y, span, stride=CHUNKS * n_tp), :] = dense[q, pl.ds(me_y * span, span), :]
+        for k in range(1, n_tp):
+            to_row(q, k).wait_recv()
+            source = lax.rem(me_y + n_tp - k, n_tp)
+            out[pl.ds(q * n_tp + source, span, stride=CHUNKS * n_tp), :] = got[q, k - 1]
+
+    for t in range(CHUNKS + 1):
+        if t < CHUNKS:
+            for q in range(SECOND + 1) if t == 0 else [t + SECOND]:
+                start_second(q)
+            start_first(t + FIRST)
+            start_direct(t + DIRECT)
+        if t > 0:
+            q = t - 1
+            stay(q).wait()
+            for f in others:
+                arrival(q, f).wait_recv()
+            if t < CHUNKS:
+                expand(q, 0, n_tp)
+                if q == 0:
+                    for y in range(n_tp):
+                        mark(q, y)
+                for k in range(1, n_tp):
+                    to_row(q, k).start()
+            else:
+                for k in [n_tp // 2] + [k for k in range(1, n_tp) if k != n_tp // 2]:
+                    expand(q, lax.rem(me_y + k, n_tp), 1)
+                    to_row(q, k).start()
+                expand(q, me_y, 1)
+            if q > 1:
+                place(q - 2)
+    for q in range(CHUNKS - 2, CHUNKS):
+        place(q)
+
+    for k in range(n_f - 1):
+        table_to(k).wait_send()
+    for q in range(CHUNKS):
+        for j in range(len(near)):
+            direct(q, j).wait_send()
+        for c in range(CORES):
+            first_leg(q, c).wait_send()
+            second_leg(q, c).wait_send()
+        for k in range(1, n_tp):
+            to_row(q, k).wait_send()
+
+
+def exchange_compact(comp, table, n_x, n_tp, rows):
+    _, span, chunk, size = layout(rows, n_tp)
+    n_f = n_x * CORES
+    dma = pltpu.SemaphoreType.DMA
+    out, _ = pl.pallas_call(
+        functools.partial(star_kernel, rows, n_x, n_tp),
+        out_shape=(
+            jax.ShapeDtypeStruct((CHUNKS * chunk, LANES), jnp.float32),
+            jax.ShapeDtypeStruct((n_f * size,), jnp.int32),
+        ),
+        in_specs=[pl.BlockSpec(memory_space=pl.ANY)] * 2,
+        out_specs=(pl.BlockSpec(memory_space=pltpu.VMEM), pl.BlockSpec(memory_space=pl.ANY)),
+        scratch_shapes=[pltpu.VMEM((n_f, CAPACITY, LANES), jnp.float32) for _ in range(CHUNKS)]
+        + [
+            pltpu.VMEM((CHUNKS, CORES, CAPACITY, LANES), jnp.float32),
+            pltpu.VMEM((CHUNKS, chunk, LANES), jnp.float32),
+            pltpu.VMEM((CHUNKS, n_tp - 1, span, LANES), jnp.float32),
+            pltpu.SMEM((n_f * size,), jnp.int32),
+            dma((3, n_f)),
+            dma((CHUNKS, 5)),
+            dma((CHUNKS, n_f)),
+            dma((2, CHUNKS, CORES)),
+            dma((CHUNKS, CORES)),
+            dma((2, CHUNKS, n_tp - 1)),
+        ],
+        compiler_params=pltpu.CompilerParams(
+            collective_id=1, has_side_effects=True, vmem_limit_bytes=40 * 1024 * 1024
+        ),
+        name="exchange_compact",
+    )(comp, table)
+    return out
+
+
 def solution(mesh):
     row_spec = P(("dp", "fsdp"), None)
     act_spec = P(("dp", "fsdp"), None, None)
@@ -289,8 +655,19 @@
 
     def local_step(tokens, out_grad, head_grad, master_w, moment_m, moment_v, learn_rate, clip_scale):
         rows = master_w.shape[0]
-        part = class_sums(tokens, out_grad, n_tp, rows)
-        embed_grad = reduce_and_place(part, n_x, n_tp, rows)
-        return adafactor_update(embed_grad, head_grad, master_w, moment_m, moment_v, learn_rate, clip_scale)
+        state = (head_grad, master_w, moment_m, moment_v, learn_rate, clip_scale)
+        keys, over = sorted_keys(tokens, n_tp, rows)
+        comp, table = compact_sums(keys, over, tokens, out_grad, n_tp, rows)
+        placed = exchange_compact(comp, table, n_x, n_tp, rows)
+        _, span, _, _ = layout(rows, n_tp)
+        first = (span - 1) * CHUNKS * n_tp
+
+        def dense(placed):
+            own_keys = keys + (placed[first, 0] < 0.0).astype(jnp.int32)
+            part = class_sums(own_keys, tokens, out_grad, n_tp, rows)
+            return jnp.pad(reduce_and_place(part, n_x, n_tp, rows), ((0, placed.shape[0] - rows), (0, 0)))
+
+        placed = lax.while_loop(lambda g: jnp.sum(g[first : first + n_tp, 0]) > 0.0, dense, placed)
+        return adafactor_update(placed[:rows], *state)
 
     return jax.shard_map(local_step, mesh=mesh, in_specs=(row_spec, act_spec, table_spec, table_spec, table_spec, table_spec, P(), P()), out_specs=(table_spec, table_spec, table_spec, table_spec), check_vma=False)

time: 252 us -> 222 us (0.88)
  Pallas kernels: 209 us -> 178 us
    pallas_call x2 -> x3, Pallas kernels: 209 us -> 178 us  [the longest x1 126 us: exchange_compact(): pl.pallas_call(functools.partial(star_kernel, rows, n_x, n_tp), out_shape...]
where the time goes in v2:
time: 222 us; the launch traced here: 221 us
  Pallas kernels  178 us (80%)
  other arithmetic  39.4 us (18%)
    pallas_call x1, Pallas kernels, exchange_compact(): pl.pallas_call(functools.partial(star_kernel, rows, n_x, n_tp), out_shape...  126 us
    pallas_call x1, Pallas kernels, compact_sums(): pl.pallas_call(functools.partial(compact_kernel, rows, n_tp), out_shape=(...  49.8 us
    convert_element_type x1, other arithmetic, adafactor_update(): return (new_w, new_m, new_v, new_w.astype(jnp.bfloat16))  13.3 us
    sort x1, other arithmetic, sorted_keys(): return (lax.sort(key.reshape(-1)), over)  12.3 us
    sort x1, other arithmetic, sorted_keys(): lax.sort((place * n_seq + lax.broadcasted_iota(jnp.int32, tokens.shape, 0...  11.2 us

profile of v2, /device:TPU:97, one launch (start us, length us, event | category | flops | bytes accessed | tf_op | source)
XLA Modules:
  0.0 221.1 jit_solution(10514873302664467875)
XLA Ops:
  0.6 1.3 fusion.7
  2.0 11.2 %sort.21 = (s32[32768]{0:T(1024)}, s32[32768]{0:T(1024)}) sort(s32[32768]{0:T(1024)S(1)} %bitcast.12, s32[32768]{0:T(1024)S(1)} %iota.12), dimensions={0}, to_apply=%region_0.1 | sort | flops 491520 | bytes 524288 | tf_op jit(solution)/shard_map/sort | solution.py:348
  13.2 2.1 slots.1
  15.3 12.3 %sort.28 = (s32[32768]{0:T(1024)S(1)}, s32[32768]{0:T(1024)}) sort(s32[32768]{0:T(1024)} %bitcast.14, s32[32768]{0:T(1024)S(1)} %iota.13), dimensions={0}, to_apply=%region_1.2 | sort | flops 491520 | bytes 524288 | tf_op jit(solution)/shard_map/sort | solution.py:355
  27.7 0.0 copy-start
  27.7 0.8 copy-done
  28.4 49.8 %compact_sums.1 = (f32[8,2176,128]{2,1,0:T(8,128)S(1)}, s32[8192]{0:T(1024)S(1)}) custom-call(s32[32768]{0:T(1024)S(1)} %get-tuple-element.110.key_ref, s32[1]{0:T(128)} %get-tuple-element.67.over_ref, s32[16,2048]{1,0:T(8,128)} %tok_ref.1, s32[16,8,256]{2,1,0:T(8,128)S(1)} %reshape.37.list_ref, bf16[16,2048,1024]{2,1,0:T(8,128)(2,1)} %x_ref.1, s32[9216]{0:T(1024)S(1)} %copy-done), custom_call_target="tpu_custom_call" | custom-call | tf_op jit(solution)/shard_map/compact_sums/pallas_call | solution.py:417
  78.2 0.0 copy-start.2
  78.2 126.2 %exchange_compact.1 = (f32[8192,128]{1,0:T(8,128)}, s32[65536]{0:T(1024)}) custom-call(f32[8,2176,128]{2,1,0:T(8,128)S(1)} %get-tuple-element.68.comp, s32[8192]{0:T(1024)S(1)} %get-tuple-element.69.table), custom_call_target="tpu_custom_call" | custom-call | tf_op jit(solution)/shard_map/exchange_compact/pallas_call | solution.py:620
  204.5 0.0 copy-done.2
  204.5 1.9 while.10
  204.5 1.3 slice_reduce_fusion.1
  207.7 13.3 %fusion.16 = (bf16[8032,128]{1,0:T(8,128)(2,1)}, f32[8032,128]{1,0:T(8,128)}, f32[8032,128]{1,0:T(8,128)}, f32[8032,128]{1,0:T(8,128)}) fusion(f32[8032,128]{1,0:T(8,128)} %param.14, f32[]{:T(128)S(6)} %mul.85, f32[]{:T(128)S(6)} %copy.17, f32[8032,128]{1,0:T(8,128)} %param.13, f32[8192,128]{1,0:T(8,128)} %get-tuple-element.71, f32[]{:T(128)S(6)} %copy.18, ...), kind=kLoop, calls=%fused_computation.38 | loop fusion | flops 16449536 | bytes 34955276 | tf_op jit(solution)/shard_map/convert_element_type | solution.py:40
  (4 shorter events, 0.1 us)
Async XLA Ops:
  27.7 0.8 copy-start
  78.2 126.3 %copy-start.2 = (s32[16,2048]{1,0:T(8,128)S(1)}, s32[16,2048]{1,0:T(8,128)}, u32[]{:S(2)}) copy-start(s32[16,2048]{1,0:T(8,128)} %tok_ref.1) | copy-start | bytes 393220
